TPU v7x, 128 devices: a whole 4x4x4 slice. The times are simulated.
128 devices in a mesh: ep: 32 (over z, x, core), dp: 4 (over y).
Axes of the slice: x: 4, y: 4, z: 4, core: 2. Of those that a mesh axis runs over, the one named last changes fastest.
Arguments:
- grad_out: float32 [16384, 1536], P(('ep', 'dp')), may hold values from -6 to 6
- tokens: bfloat16 [16384, 1536], P(('ep', 'dp')), may hold values from -6 to 6
- probs: float32 [16384, 4], P(('ep', 'dp')), may hold values from 0.1 to 0.5
- expert_ids: int32 [16384, 4], P(('ep', 'dp')), may hold values from 0 to 31, all different within a row; in each aligned block of 128 rows (0 to 127, 128 to 255, ...) at most 20 rows name the same one
- priority: int32 [128, 128], P(('ep', 'dp')), may hold values from 0 to 127, each once within a row
- cap_counts: int32 [32], replicated, may hold values from 10 to 20, as said below
- gate_weight: bfloat16 [32, 1536, 1536], P('ep'), may hold values from -0.15625 to 0.15625
- up_weight: bfloat16 [32, 1536, 1536], P('ep'), may hold values from -0.15625 to 0.15625
- down_weight: bfloat16 [32, 1536, 1536], P('ep'), may hold values from -0.15625 to 0.15625
Outputs:
- input_grad: bfloat16 [16384, 1536], P(('ep', 'dp'))
- prob_grad: float32 [16384, 4], P(('ep', 'dp'))
- gate_grad: bfloat16 [32, 1536, 1536], P('ep', 'dp')
- up_grad: bfloat16 [32, 1536, 1536], P('ep', 'dp')
- down_grad: bfloat16 [32, 1536, 1536], P('ep', 'dp')
Inputs may be any that keep to these rules, and one draw needn't show every extreme that they name: `expert_ids`: each row names 4 different experts; among the rows of one device no expert is named by more than 20 rows, and in some device some expert is named by exactly 20 rows. `priority`: each row orders the 128 tokens of one device, each number once. `cap_counts`: some expert has exactly 20.
All inputs are finite; a program needn't handle non-finite values. Where the computation divides by a largest or mean magnitude, that divisor is 1e-20 or more.
Results may differ from a plain program's by a relative error of at most 0.017.
Values may be sent and summed in bfloat16 or wider, within the bound.
A program may use at most 128 MiB of HBM per device.

v0:
```python
import jax
import jax.numpy as jnp
from jax import lax
from jax.sharding import PartitionSpec as P

sharpness = 1.702


def contract_last(first_op, second_op):
    return lax.dot_general(
        first_op, second_op, (((1,), (1,)), ((), ())), preferred_element_type=jnp.float32
    )


def contract_first(first_op, second_op):
    return lax.dot_general(
        first_op, second_op, (((0,), (0,)), ((), ())), preferred_element_type=jnp.float32
    )


def route_table(expert_ids, priority, cap_counts, buckets, capacity):
    ranking = priority[0]
    earlier = (ranking[None, :] < ranking[:, None]).astype(jnp.float32)
    expert_range = lax.broadcasted_iota(jnp.int32, (1, 1, buckets), 2)
    matches = (expert_ids[:, :, None] == expert_range).astype(jnp.float32)
    routed = jnp.sum(matches, axis=1)
    before = jnp.dot(earlier, routed)
    slot_rank = jnp.sum(matches * before[:, None, :], axis=2)
    keep_limit = jnp.sum(matches * cap_counts.astype(jnp.float32)[None, None, :], axis=2)
    slot_range = lax.broadcasted_iota(jnp.float32, (1, 1, capacity), 2)
    slot_hit = (
        (slot_rank[:, :, None] == slot_range) & (slot_rank < keep_limit)[:, :, None]
    ).astype(jnp.float32)
    placement = matches[:, :, :, None] * slot_hit[:, :, None, :]
    return placement.reshape(expert_ids.shape[0], expert_ids.shape[1], buckets * capacity)


def deltas(slot_x, slot_g, w_gate, w_up, w_down):
    gate_pre = contract_last(slot_x, w_gate)
    up_pre = contract_last(slot_x, w_up)
    act_delta = contract_last(slot_g, w_down)
    squash = jax.nn.sigmoid(sharpness * gate_pre)
    gated = gate_pre * squash
    activated = (up_pre + 1.0) * gated
    up_delta = (act_delta * gated).astype(jnp.bfloat16)
    gate_delta = (
        act_delta * (up_pre + 1.0) * (squash + sharpness * gate_pre * squash * (1.0 - squash))
    ).astype(jnp.bfloat16)
    return (activated, act_delta, gate_delta, up_delta)


def on_device(
    grad_out, tokens, probs, expert_ids, priority, cap_counts, gate_weight, up_weight, down_weight
):
    ep_size = lax.axis_size("ep")
    dp_size = lax.axis_size("dp")
    tok_rows, model_width = tokens.shape
    route_count = expert_ids.shape[1]
    capacity = 5 * route_count * tok_rows // (4 * ep_size)
    slot_rows = ep_size * capacity
    placement = route_table(expert_ids, priority, cap_counts, ep_size, capacity)
    slot_table = jnp.sum(placement, axis=1)
    table_low = slot_table.astype(jnp.bfloat16)
    row_scale = jnp.maximum(jnp.max(jnp.abs(grad_out), axis=1), 1.0)
    quantized = (grad_out / row_scale[:, None]).astype(jnp.bfloat16)
    send_prob = jnp.sum(placement * probs[:, :, None], axis=(0, 1))
    send_scale = jnp.sum(slot_table * row_scale[:, None], axis=0)
    send_x = jnp.einsum("ts,td->sd", table_low, tokens, preferred_element_type=jnp.float32).astype(
        jnp.bfloat16
    )
    send_g = (
        jnp.einsum("ts,td->sd", table_low, quantized, preferred_element_type=jnp.float32)
        * (send_prob * send_scale)[:, None]
    ).astype(jnp.bfloat16)
    bucket_shape = (ep_size, capacity, model_width)

    def exchange(a):
        return lax.all_to_all(a, "ep", split_axis=0, concat_axis=0, tiled=True)

    slot_x = exchange(send_x.reshape(bucket_shape)).reshape(slot_rows, model_width)
    all_x = lax.all_gather(slot_x, "dp", axis=0, tiled=True)
    slot_g = exchange(send_g.reshape(bucket_shape)).reshape(slot_rows, model_width)
    all_g = lax.all_gather(slot_g, "dp", axis=0, tiled=True)
    w_gate = gate_weight[0]
    w_up = up_weight[0]
    w_down = down_weight[0]
    activated, act_delta, gate_delta, up_delta = deltas(slot_x, slot_g, w_gate, w_up, w_down)
    slot_in = (
        jnp.dot(gate_delta, w_gate, preferred_element_type=jnp.float32)
        + jnp.dot(up_delta, w_up, preferred_element_type=jnp.float32)
    ).astype(jnp.bfloat16)
    slot_out = jnp.sum(activated * act_delta, axis=1)
    back_in = exchange(slot_in.reshape(bucket_shape))
    back_prob = exchange(slot_out.reshape(ep_size, capacity).astype(jnp.bfloat16))
    prob_grad = jnp.einsum("tks,s->tk", placement, back_prob.reshape(slot_rows)) / probs
    input_grad = jnp.einsum(
        "ts,sd->td",
        table_low,
        back_in.reshape(slot_rows, model_width),
        preferred_element_type=jnp.float32,
    ).astype(jnp.bfloat16)
    share = w_gate.shape[0] // dp_size
    first = lax.axis_index("dp") * share

    def mine(w):
        return lax.dynamic_slice_in_dim(w, first, share, 0)

    act_mine, _, gd_mine, ud_mine = deltas(all_x, all_g, mine(w_gate), mine(w_up), mine(w_down))
    gate_share = contract_first(gd_mine, all_x).astype(jnp.bfloat16)
    up_share = contract_first(ud_mine, all_x).astype(jnp.bfloat16)
    down_share = contract_first(act_mine.astype(jnp.bfloat16), all_g).astype(jnp.bfloat16)
    return (input_grad, prob_grad, gate_share[None], up_share[None], down_share[None])


def solution(mesh):
    return jax.shard_map(
        on_device,
        mesh=mesh,
        in_specs=(
            P(("ep", "dp"), None),
            P(("ep", "dp"), None),
            P(("ep", "dp"), None),
            P(("ep", "dp"), None),
            P(("ep", "dp"), None),
            P(),
            P("ep", None, None),
            P("ep", None, None),
            P("ep", None, None),
        ),
        out_specs=(
            P(("ep", "dp"), None),
            P(("ep", "dp"), None),
            P("ep", "dp", None),
            P("ep", "dp", None),
            P("ep", "dp", None),
        ),
        check_vma=False,
    )
```

profile of v0, /device:TPU:1, one launch (start us, length us, event | category | flops | bytes accessed | tf_op | source)
XLA Modules:
  0.0 248.0 jit_solution(7221112332950681031)
XLA Ops:
  13.6 1.9 convolution_convert_fusion
  15.6 2.5 reshape.94
  18.0 40.7 %all_to_all.24 = bf16[32,20,1536]{2,1,0:T(8,128)(2,1)} all-to-all(bf16[32,20,1536]{2,1,0:T(8,128)(2,1)S(1)} %reshape.94), channel_id=1, replica_groups=mesh['ep'=32,'dp'=4] {'ep'}, dimensions={0} | all-to-all | bytes 3932160 | tf_op jit(solution)/shard_map/all_to_all | solution.py:78
  58.7 4.1 %reshape.95 = bf16[640,1536]{1,0:T(8,128)(2,1)} reshape(bf16[32,20,1536]{2,1,0:T(8,128)(2,1)} %all_to_all.24) | data formatting | bytes 3932160 | tf_op jit(solution)/shard_map/reshape | solution.py:80
  63.1 2.1 multiply_convert_fusion.5
  65.2 2.5 reshape.92
  67.6 35.0 %all_to_all.25 = bf16[32,20,1536]{2,1,0:T(8,128)(2,1)} all-to-all(bf16[32,20,1536]{2,1,0:T(8,128)(2,1)S(1)} %reshape.92), channel_id=1, replica_groups=mesh['ep'=32,'dp'=4] {'ep'}, dimensions={0} | all-to-all | bytes 3932160 | tf_op jit(solution)/shard_map/all_to_all | solution.py:78
  102.6 4.1 %reshape.93 = bf16[640,1536]{1,0:T(8,128)(2,1)} reshape(bf16[32,20,1536]{2,1,0:T(8,128)(2,1)} %all_to_all.25) | data formatting | bytes 3932160 | tf_op jit(solution)/shard_map/reshape | solution.py:82
  106.8 5.3 %fusion.6 = f32[640,1536]{1,0:T(8,128)S(1)} fusion(bf16[640,1536]{1,0:T(8,128)(2,1)S(1)} %copy-done.2, bf16[1,1536,1536]{2,1,0:T(8,128)(2,1)} %param.16), kind=kOutput, calls=%fused_computation.6 | convolution fusion | flops 3019898880 | bytes 10616832 | tf_op jit(solution)/shard_map/dot_general | solution.py:10
  112.1 6.6 %fusion.2 = f32[640,1536]{1,0:T(8,128)S(1)} fusion(bf16[640,1536]{1,0:T(8,128)(2,1)S(1)} %copy-done.2, bf16[1,1536,1536]{2,1,0:T(8,128)(2,1)} %param.15), kind=kOutput, calls=%fused_computation.2 | convolution fusion | flops 3019898880 | bytes 10616832 | tf_op jit(solution)/shard_map/dot_general | solution.py:10
  118.8 5.4 %multiply_reduce_fusion = (bf16[640]{0:T(1024)(128)(2,1)S(1)}, f32[640,1536]{1,0:T(8,128)}) fusion(f32[640,1536]{1,0:T(8,128)S(1)} %fusion.6, f32[640,1536]{1,0:T(8,128)S(1)} %fusion.2, bf16[640,1536]{1,0:T(8,128)(2,1)S(1)} %copy-done.3, bf16[1,1536,1536]{2,1,0:T(8,128)(2,1)S(1)} %bitcast.64), kind=kOutput, calls=%fused_computation.15 | convolution fusion | flops 3028745728 | bytes 18482432 | tf_op jit(solution)/shard_map/dot_general | solution.py:10
  124.9 3.8 %all-to-all-start.3 = ((bf16[32,1,20]{2,1,0:T(2,128)(2,1)}), bf16[32,1,20]{2,1,0:T(2,128)(2,1)S(1)}, u32[]{:S(2)}, u32[]{:S(2)}) async-start(bf16[32,1,20]{2,1,0:T(2,128)(2,1)} %convert_element_type.97), calls=%async_computation.3 | async-start | bytes 32768 | tf_op jit(solution)/shard_map/all_to_all | solution.py:78
  128.8 8.9 %fusion = f32[640,1536]{1,0:T(8,128)S(1)} fusion(bf16[1,1536,1536]{2,1,0:T(8,128)(2,1)} %param.15, f32[640,1536]{1,0:T(8,128)} %get-tuple-element.12, f32[640,1536]{1,0:T(8,128)} %copy-done.9, f32[640,1536]{1,0:T(8,128)} %copy-done.11), kind=kOutput, calls=%fused_computation | convolution fusion | flops 3031695360 | bytes 20447232 | tf_op jit(solution)/shard_map/dot_general | solution.py:89
  137.7 5.8 %add_convert_fusion = bf16[640,1536]{1,0:T(8,128)(2,1)S(1)} fusion(f32[640,1536]{1,0:T(8,128)S(1)} %fusion, bf16[1,1536,1536]{2,1,0:T(8,128)(2,1)} %param.16, f32[640,1536]{1,0:T(8,128)S(1)} %copy-done.13, f32[640,1536]{1,0:T(8,128)S(1)} %copy-done.10), kind=kOutput, calls=%fused_computation.16 | convolution fusion | flops 3028746240 | bytes 18481152 | tf_op jit(solution)/shard_map/dot_general | solution.py:90
  143.6 2.1 reshape.96
  145.7 7.3 %all-to-all-start.2 = ((bf16[32,20,1536]{2,1,0:T(8,128)(2,1)}), bf16[32,20,1536]{2,1,0:T(8,128)(2,1)S(1)}, u32[]{:S(2)}, u32[]{:S(2)}) async-start(bf16[32,20,1536]{2,1,0:T(8,128)(2,1)} %reshape.96), calls=%async_computation.2 | async-start | bytes 4718592 | tf_op jit(solution)/shard_map/all_to_all | solution.py:78
  154.0 30.6 %all-to-all-done.2 = bf16[32,20,1536]{2,1,0:T(8,128)(2,1)S(1)} async-done(((bf16[32,20,1536]{2,1,0:T(8,128)(2,1)}), bf16[32,20,1536]{2,1,0:T(8,128)(2,1)S(1)}, u32[]{:S(2)}, u32[]{:S(2)}) %all-to-all-start.2) | async-done | bytes 1966112 | tf_op jit(solution)/shard_map/all_to_all | solution.py:78
  186.1 9.9 %fusion.25 = f32[2560,384]{1,0:T(8,128)} fusion(bf16[2560,1536]{1,0:T(8,128)(2,1)} %all-gather.5.cloned.1.call-done, bf16[1,1536,1536]{2,1,0:T(8,128)(2,1)} %param.15, s32[]{:T(128)S(6)} %select_n.2), kind=kOutput, calls=%fused_computation.41 | convolution fusion | flops 3019898880 | bytes 12976132 | tf_op jit(solution)/shard_map/dot_general | solution.py:10
  196.0 7.5 %convolution_add_fusion = f32[2560,384]{1,0:T(8,128)} fusion(bf16[2560,1536]{1,0:T(8,128)(2,1)S(1)} %copy-done.6, bf16[1,1536,1536]{2,1,0:T(8,128)(2,1)} %param.16, s32[]{:T(128)S(6)} %select_n.2), kind=kOutput, calls=%fused_computation.10 | convolution fusion | flops 3020881920 | bytes 12976132 | tf_op jit(solution)/shard_map/dot_general | solution.py:10
  203.4 16.9 %all-gather.3.cloned.1.call-done = bf16[2560,1536]{1,0:T(8,128)(2,1)} async-done(((bf16[640,1536]{1,0:T(8,128)(2,1)}), bf16[2560,1536]{1,0:T(8,128)(2,1)}) %all-gather.3.cloned.1.call-update) | async-done | bytes 7864336 | tf_op jit(solution)/shard_map/all_gather | solution.py:83
  220.3 7.4 %fusion.28 = f32[2560,384]{1,0:T(8,128)S(1)} fusion(bf16[2560,1536]{1,0:T(8,128)(2,1)} %all-gather.3.cloned.1.call-done, bf16[1,1536,1536]{2,1,0:T(8,128)(2,1)} %param.17, s32[]{:T(128)S(6)} %select_n.2), kind=kOutput, calls=%fused_computation.44 | convolution fusion | flops 3019898880 | bytes 12976132 | tf_op jit(solution)/shard_map/dot_general | solution.py:10
  227.7 4.4 %fusion.15 = bf16[1,384,1536]{2,1,0:T(8,128)(2,1)} fusion(bf16[2560,1536]{1,0:T(8,128)(2,1)S(1)} %copy-done.7, f32[2560,384]{1,0:T(8,128)S(1)} %fusion.28, f32[2560,384]{1,0:T(8,128)S(1)} %copy-done.8), kind=kOutput, calls=%fused_computation.28 | convolution fusion | flops 3027369984 | bytes 16908288 | tf_op jit(solution)/shard_map/dot_general | solution.py:16
  232.2 4.5 %fusion.14 = bf16[1,384,1536]{2,1,0:T(8,128)(2,1)} fusion(bf16[2560,1536]{1,0:T(8,128)(2,1)S(1)} %copy-done.7, f32[2560,384]{1,0:T(8,128)S(1)} %fusion.28, f32[2560,384]{1,0:T(8,128)S(1)} %copy-done.12, f32[2560,384]{1,0:T(8,128)S(1)} %copy-done.8), kind=kOutput, calls=%fused_computation.27 | convolution fusion | flops 3031302144 | bytes 20840448 | tf_op jit(solution)/shard_map/dot_general | solution.py:16
  236.7 4.4 %fusion.16 = bf16[1,384,1536]{2,1,0:T(8,128)(2,1)} fusion(bf16[2560,1536]{1,0:T(8,128)(2,1)S(1)} %bitcast.62, f32[2560,384]{1,0:T(8,128)S(1)} %copy-done.12, f32[2560,384]{1,0:T(8,128)S(1)} %copy-done.8), kind=kOutput, calls=%fused_computation.29 | convolution fusion | flops 3027369984 | bytes 16908288 | tf_op jit(solution)/shard_map/dot_general | solution.py:16
  (65 shorter events, 9.9 us)
Async XLA Ops:
  7.2 6.5 %copy-start = (bf16[128,1536]{1,0:T(8,128)(2,1)S(1)}, bf16[128,1536]{1,0:T(8,128)(2,1)}, u32[]{:S(2)}) copy-start(bf16[128,1536]{1,0:T(8,128)(2,1)} %param.10) | copy-start | bytes 1179652
  7.2 178.9 %all-gather.5.cloned.1.call-start = ((), (), s32[]{:S(2)}) async-start(), calls=%async_computation.5 | async-start | bytes 9830400 | tf_op jit(solution)/shard_map/all_gather | solution.py:81
  58.7 4.3 %copy-start.4 = (f32[128,1536]{1,0:T(8,128)S(1)}, f32[128,1536]{1,0:T(8,128)}, u32[]{:S(2)}) copy-start(f32[128,1536]{1,0:T(8,128)} %param.9) | copy-start | bytes 2359300
  62.8 157.5 %all-gather.3.cloned.1.call-start = ((), (), s32[]{:S(2)}) async-start(), calls=%async_computation.4 | async-start | bytes 9830400 | tf_op jit(solution)/shard_map/all_gather | solution.py:83
  102.6 4.2 %copy-start.2 = (bf16[640,1536]{1,0:T(8,128)(2,1)S(1)}, bf16[640,1536]{1,0:T(8,128)(2,1)}, u32[]{:S(2)}) copy-start(bf16[640,1536]{1,0:T(8,128)(2,1)} %reshape.95) | copy-start | bytes 5898244
  106.8 12.0 %slice-start.2 = ((s8[4718592]{0:T(1024)(128)(4,1)}), s8[4194304]{0:T(1024)(128)(4,1)S(1)}, s32[]{:S(2)}) async-start(s8[4718592]{0:T(1024)(128)(4,1)} %bitcast.63), calls=%async_computation.8 | async-start | bytes 8388608
  112.1 6.7 %copy-start.11 = (f32[640,1536]{1,0:T(8,128)}, f32[640,1536]{1,0:T(8,128)S(1)}, u32[]{:S(2)}) copy-start(f32[640,1536]{1,0:T(8,128)S(1)} %fusion.6) | copy-start | bytes 11796484
  112.1 6.7 %copy-start.3 = (bf16[640,1536]{1,0:T(8,128)(2,1)S(1)}, bf16[640,1536]{1,0:T(8,128)(2,1)}, u32[]{:S(2)}) copy-start(bf16[640,1536]{1,0:T(8,128)(2,1)} %reshape.93) | copy-start | bytes 5898244
  112.1 6.7 %slice-start.3 = ((s8[4718592]{0:T(1024)(128)(4,1)}), s8[524288]{0:T(1024)(128)(4,1)S(1)}, s32[]{:S(2)}) async-start(s8[4718592]{0:T(1024)(128)(4,1)} %bitcast.63), calls=%async_computation.9 | async-start | bytes 1048576
  118.8 5.4 %copy-start.9 = (f32[640,1536]{1,0:T(8,128)}, f32[640,1536]{1,0:T(8,128)S(1)}, u32[]{:S(2)}) copy-start(f32[640,1536]{1,0:T(8,128)S(1)} %fusion.2) | copy-start | bytes 11796484
  124.9 20.7 %all-to-all-start.3 = ((bf16[32,1,20]{2,1,0:T(2,128)(2,1)}), bf16[32,1,20]{2,1,0:T(2,128)(2,1)S(1)}, u32[]{:S(2)}, u32[]{:S(2)}) async-start(bf16[32,1,20]{2,1,0:T(2,128)(2,1)} %convert_element_type.97), calls=%async_computation.3 | async-start | bytes 32768 | tf_op jit(solution)/shard_map/all_to_all | solution.py:78
  128.8 9.0 %copy-start.10 = (f32[640,1536]{1,0:T(8,128)S(1)}, f32[640,1536]{1,0:T(8,128)}, u32[]{:S(2)}) copy-start(f32[640,1536]{1,0:T(8,128)} %copy-done.9) | copy-start | bytes 11796484
  128.8 9.0 %copy-start.13 = (f32[640,1536]{1,0:T(8,128)S(1)}, f32[640,1536]{1,0:T(8,128)}, u32[]{:S(2)}) copy-start(f32[640,1536]{1,0:T(8,128)} %get-tuple-element.12) | copy-start | bytes 11796484
  143.6 9.8 %copy-start.5 = (f32[128,4]{0,1:T(4,128)S(1)}, f32[128,4]{0,1:T(4,128)}, u32[]{:S(2)}) copy-start(f32[128,4]{0,1:T(4,128)} %param.11) | copy-start | bytes 6148
  145.7 38.9 %all-to-all-start.2 = ((bf16[32,20,1536]{2,1,0:T(8,128)(2,1)}), bf16[32,20,1536]{2,1,0:T(8,128)(2,1)S(1)}, u32[]{:S(2)}, u32[]{:S(2)}) async-start(bf16[32,20,1536]{2,1,0:T(8,128)(2,1)} %reshape.96), calls=%async_computation.2 | async-start | bytes 4718592 | tf_op jit(solution)/shard_map/all_to_all | solution.py:78
  186.1 9.9 %copy-start.6 = (bf16[2560,1536]{1,0:T(8,128)(2,1)S(1)}, bf16[2560,1536]{1,0:T(8,128)(2,1)}, u32[]{:S(2)}) copy-start(bf16[2560,1536]{1,0:T(8,128)(2,1)} %all-gather.5.cloned.1.call-done) | copy-start | bytes 23592964
  220.3 7.4 %copy-start.7 = (bf16[2560,1536]{1,0:T(8,128)(2,1)S(1)}, bf16[2560,1536]{1,0:T(8,128)(2,1)}, u32[]{:S(2)}) copy-start(bf16[2560,1536]{1,0:T(8,128)(2,1)} %all-gather.5.cloned.1.call-done) | copy-start | bytes 23592964
  220.3 7.4 %copy-start.8 = (f32[2560,384]{1,0:T(8,128)S(1)}, f32[2560,384]{1,0:T(8,128)}, u32[]{:S(2)}) copy-start(f32[2560,384]{1,0:T(8,128)} %fusion.25) | copy-start | bytes 11796484
  227.7 4.5 %copy-start.12 = (f32[2560,384]{1,0:T(8,128)S(1)}, f32[2560,384]{1,0:T(8,128)}, u32[]{:S(2)}) copy-start(f32[2560,384]{1,0:T(8,128)} %convolution_add_fusion) | copy-start | bytes 11796484
  227.7 9.0 %slice-start = ((s8[7864320]{0:T(1024)(128)(4,1)}), s8[4194304]{0:T(1024)(128)(4,1)S(1)}, s32[]{:S(2)}) async-start(s8[7864320]{0:T(1024)(128)(4,1)} %bitcast.61), calls=%async_computation.6 | async-start | bytes 8388608
  232.2 4.6 %slice-start.1 = ((s8[7864320]{0:T(1024)(128)(4,1)}), s8[3670016]{0:T(1024)(128)(4,1)S(1)}, s32[]{:S(2)}) async-start(s8[7864320]{0:T(1024)(128)(4,1)} %bitcast.61), calls=%async_computation.7 | async-start | bytes 7340032
  236.7 4.4 %copy-start.1 = (bf16[128,1536]{1,0:T(8,128)(2,1)S(1)}, bf16[128,1536]{1,0:T(8,128)(2,1)}, u32[]{:S(2)}) copy-start(bf16[128,1536]{1,0:T(8,128)(2,1)} %param.10) | copy-start | bytes 1179652
Sparse Core Ops, SparseCore 0:
  62.9 76.0 all-gather.4
  140.7 79.5 all-gather.2
where the time goes:
time: 249 us; the launch traced here: 248 us
  matrix products  76.9 us (31%)
  blocking collectives  75.7 us (30%)
  waiting for transfers between devices  47.5 us (19%)
  local copies, waits for them, and re-layouts  16.4 us (7%)
  between operations  14.4 us (6%)
  starting transfers between devices  11.2 us (4%)
  other arithmetic  5.9 us (2%)
    all_to_all x2, blocking collectives, exchange(): return lax.all_to_all(a, 'ep', split_axis=0, concat_axis=0, tiled=True)  75.7 us
    dot_general x6, matrix products, contract_last(): lax.dot_general(first_op, second_op, (((1,), (1,)), ((), ())), preferred_...  42 us
    all_to_all x2, waiting for transfers between devices, exchange(): return lax.all_to_all(a, 'ep', split_axis=0, concat_axis=0, tiled=True)  30.6 us
    all_gather x1, waiting for transfers between devices, on_device(): all_g = lax.all_gather(slot_g, 'dp', axis=0, tiled=True)  16.9 us
    dot_general x3, matrix products, contract_first(): lax.dot_general(first_op, second_op, (((0,), (0,)), ((), ())), preferred_...  13.4 us
    all_to_all x2, starting transfers between devices, exchange(): return lax.all_to_all(a, 'ep', split_axis=0, concat_axis=0, tiled=True)  11.1 us
    dot_general x1, matrix products, on_device(): jnp.dot(gate_delta, w_gate, preferred_element_type=jnp.float32)  8.95 us
    dot_general x1, matrix products, on_device(): jnp.dot(up_delta, w_up, preferred_element_type=jnp.float32)  5.8 us
  transfers between devices with their start and end apart: 4, of which 2 were waited for; matrix products, arithmetic and copies ran while one was open for 26% of the time, Pallas kernels for 0%

commit v1 on v0

--- a/solution.py
+++ b/solution.py
@@ -80,7 +80,9 @@
     slot_x = exchange(send_x.reshape(bucket_shape)).reshape(slot_rows, model_width)
     all_x = lax.all_gather(slot_x, "dp", axis=0, tiled=True)
     slot_g = exchange(send_g.reshape(bucket_shape)).reshape(slot_rows, model_width)
-    all_g = lax.all_gather(slot_g, "dp", axis=0, tiled=True)
+    all_g = jnp.concatenate(
+        lax.all_to_all(jnp.stack([slot_g] * lax.axis_size("dp")), "dp", 0, 0), axis=0
+    )
     w_gate = gate_weight[0]
     w_up = up_weight[0]
     w_down = down_weight[0]

time: 249 us -> 318 us (1.28)
  waiting for transfers between devices: 47.5 us -> 126 us
  blocking collectives: 75.7 us -> 38.9 us
  starting transfers between devices: 11.2 us -> 27.2 us
  matrix products: 76.9 us -> 86.8 us
    all_to_all x0 -> x1, waiting for transfers between devices: none -> 85.7 us  [on_device(): lax.all_to_all(jnp.stack([slot_g] * lax.axis_size('dp')), 'dp', 0, 0)]
    all_to_all x2 -> x1, blocking collectives: 75.7 us -> 38.9 us  [exchange(): return lax.all_to_all(a, 'ep', split_axis=0, concat_axis=0, tiled=True)]
    all_gather x1 -> x0, waiting for transfers between devices: 16.9 us -> none  [on_device(): all_g = lax.all_gather(slot_g, 'dp', axis=0, tiled=True)]
    all_to_all x2 -> x3, starting transfers between devices: 11.1 us -> 21.4 us  [exchange(): return lax.all_to_all(a, 'ep', split_axis=0, concat_axis=0, tiled=True)]
    all_to_all x2 -> x3, waiting for transfers between devices: 30.6 us -> 39.9 us  [exchange(): return lax.all_to_all(a, 'ep', split_axis=0, concat_axis=0, tiled=True)]
    all_to_all x0 -> x1, starting transfers between devices: none -> 5.74 us  [on_device(): lax.all_to_all(jnp.stack([slot_g] * lax.axis_size('dp')), 'dp', 0, 0)]
    dot_general x6, matrix products: 42 us -> 47.3 us  [contract_last(): lax.dot_general(first_op, second_op, (((1,), (1,)), ((), ())), preferred_...]
    another operation x0 -> x1, local copies, waits for them, and re-layouts: none -> 3.73 us  [on_device(): jnp.stack([slot_g] * lax.axis_size('dp'))]
  transfers between devices with their start and end apart: 4 -> 5, of which waited for: 2 -> 3; matrix products, arithmetic and copies ran while one was open for 26% -> 23% of each run, Pallas kernels for 0% -> 0%
where the time goes in v1:
time: 318 us; the launch traced here: 317 us
  waiting for transfers between devices  126 us (40%)
  matrix products  86.8 us (27%)
  blocking collectives  38.9 us (12%)
  starting transfers between devices  27.2 us (9%)
  local copies, waits for them, and re-layouts  18 us (6%)
  between operations  14.3 us (4%)
  other arithmetic  5.91 us (2%)
    all_to_all x1, waiting for transfers between devices, on_device(): lax.all_to_all(jnp.stack([slot_g] * lax.axis_size('dp')), 'dp', 0, 0)  85.7 us
    dot_general x6, matrix products, contract_last(): lax.dot_general(first_op, second_op, (((1,), (1,)), ((), ())), preferred_...  47.3 us
    all_to_all x3, waiting for transfers between devices, exchange(): return lax.all_to_all(a, 'ep', split_axis=0, concat_axis=0, tiled=True)  39.9 us
    all_to_all x1, blocking collectives, exchange(): return lax.all_to_all(a, 'ep', split_axis=0, concat_axis=0, tiled=True)  38.9 us
    all_to_all x3, starting transfers between devices, exchange(): return lax.all_to_all(a, 'ep', split_axis=0, concat_axis=0, tiled=True)  21.4 us
    dot_general x3, matrix products, contract_first(): lax.dot_general(first_op, second_op, (((0,), (0,)), ((), ())), preferred_...  16.9 us
    dot_general x1, matrix products, on_device(): jnp.dot(gate_delta, w_gate, preferred_element_type=jnp.float32)  9.07 us
    dot_general x1, matrix products, on_device(): jnp.dot(up_delta, w_up, preferred_element_type=jnp.float32)  7.07 us
  transfers between devices with their start and end apart: 5, of which 3 were waited for; matrix products, arithmetic and copies ran while one was open for 23% of the time, Pallas kernels for 0%

profile of v1, /device:TPU:1, one launch (start us, length us, event | category | flops | bytes accessed | tf_op | source)
XLA Modules:
  0.0 316.6 jit_solution(16123422974308448351)
XLA Ops:
  16.3 9.4 %all-to-all-start.1 = ((bf16[32,20,1536]{2,1,0:T(8,128)(2,1)}), bf16[32,20,1536]{2,1,0:T(8,128)(2,1)S(1)}, u32[]{:S(2)}, u32[]{:S(2)}) async-start(bf16[32,20,1536]{2,1,0:T(8,128)(2,1)} %reshape.99), calls=%async_computation.1 | async-start | bytes 4718592 | tf_op jit(solution)/shard_map/all_to_all | solution.py:78
  26.0 3.2 multiply_convert_fusion.5
  29.1 4.0 %reshape.97 = bf16[32,20,1536]{2,1,0:T(8,128)(2,1)} reshape(bf16[640,1536]{1,0:T(8,128)(2,1)} %multiply_convert_fusion.5) | data formatting | bytes 3932160 | tf_op jit(solution)/shard_map/reshape | solution.py:82
  33.1 24.2 %all-to-all-done.1 = bf16[32,20,1536]{2,1,0:T(8,128)(2,1)S(1)} async-done(((bf16[32,20,1536]{2,1,0:T(8,128)(2,1)}), bf16[32,20,1536]{2,1,0:T(8,128)(2,1)S(1)}, u32[]{:S(2)}, u32[]{:S(2)}) %all-to-all-start.1) | async-done | bytes 1966112 | tf_op jit(solution)/shard_map/all_to_all | solution.py:78
  57.3 6.3 %all-to-all-start = ((bf16[32,20,1536]{2,1,0:T(8,128)(2,1)}), bf16[32,20,1536]{2,1,0:T(8,128)(2,1)}, u32[]{:S(2)}, u32[]{:S(2)}) async-start(bf16[32,20,1536]{2,1,0:T(8,128)(2,1)} %reshape.97), calls=%async_computation | async-start | bytes 4718592 | tf_op jit(solution)/shard_map/all_to_all | solution.py:78
  65.6 8.3 %fusion.6 = f32[640,1536]{1,0:T(8,128)} fusion(bf16[640,1536]{1,0:T(8,128)(2,1)} %reshape.100, bf16[1,1536,1536]{2,1,0:T(8,128)(2,1)} %param.16), kind=kOutput, calls=%fused_computation.6 | convolution fusion | flops 3019898880 | bytes 10616832 | tf_op jit(solution)/shard_map/dot_general | solution.py:10
  73.9 5.2 %fusion.2 = f32[640,1536]{1,0:T(8,128)} fusion(bf16[640,1536]{1,0:T(8,128)(2,1)S(1)} %copy-done.5, bf16[1,1536,1536]{2,1,0:T(8,128)(2,1)S(1)} %bitcast.63), kind=kOutput, calls=%fused_computation.2 | convolution fusion | flops 3019898880 | bytes 10616832 | tf_op jit(solution)/shard_map/dot_general | solution.py:10
  79.1 15.7 %all-to-all-done = bf16[32,20,1536]{2,1,0:T(8,128)(2,1)} async-done(((bf16[32,20,1536]{2,1,0:T(8,128)(2,1)}), bf16[32,20,1536]{2,1,0:T(8,128)(2,1)}, u32[]{:S(2)}, u32[]{:S(2)}) %all-to-all-start) | async-done | bytes 1966112 | tf_op jit(solution)/shard_map/all_to_all | solution.py:78
  94.8 2.6 reshape.98
  97.5 10.8 %multiply_reduce_fusion = (bf16[640]{0:T(1024)(128)(2,1)S(1)}, f32[640,1536]{1,0:T(8,128)}) fusion(f32[640,1536]{1,0:T(8,128)} %fusion.6, f32[640,1536]{1,0:T(8,128)} %fusion.2, bf16[640,1536]{1,0:T(8,128)(2,1)S(1)} %reshape.98, bf16[1,1536,1536]{2,1,0:T(8,128)(2,1)} %param.17), kind=kOutput, calls=%fused_computation.15 | convolution fusion | flops 3028745728 | bytes 18482432 | tf_op jit(solution)/shard_map/dot_general | solution.py:10
  109.0 5.7 %all-to-all-start.3 = ((bf16[32,1,20]{2,1,0:T(2,128)(2,1)}), bf16[32,1,20]{2,1,0:T(2,128)(2,1)S(1)}, u32[]{:S(2)}, u32[]{:S(2)}) async-start(bf16[32,1,20]{2,1,0:T(2,128)(2,1)} %convert_element_type.97), calls=%async_computation.3 | async-start | bytes 32768 | tf_op jit(solution)/shard_map/all_to_all | solution.py:78
  114.7 9.1 %fusion = f32[640,1536]{1,0:T(8,128)S(1)} fusion(bf16[1,1536,1536]{2,1,0:T(8,128)(2,1)} %param.15, f32[640,1536]{1,0:T(8,128)} %get-tuple-element.12, f32[640,1536]{1,0:T(8,128)} %fusion.2, f32[640,1536]{1,0:T(8,128)} %fusion.6), kind=kOutput, calls=%fused_computation | convolution fusion | flops 3031695360 | bytes 20447232 | tf_op jit(solution)/shard_map/dot_general | solution.py:91
  123.8 7.1 %add_convert_fusion = bf16[640,1536]{1,0:T(8,128)(2,1)} fusion(f32[640,1536]{1,0:T(8,128)S(1)} %fusion, bf16[1,1536,1536]{2,1,0:T(8,128)(2,1)} %param.16, f32[640,1536]{1,0:T(8,128)S(1)} %copy-done.10, f32[640,1536]{1,0:T(8,128)S(1)} %copy-done.9), kind=kOutput, calls=%fused_computation.16 | convolution fusion | flops 3028746240 | bytes 18481152 | tf_op jit(solution)/shard_map/dot_general | solution.py:92
  130.9 2.5 reshape.101
  133.4 38.9 %all_to_all.29 = bf16[32,20,1536]{2,1,0:T(8,128)(2,1)} all-to-all(bf16[32,20,1536]{2,1,0:T(8,128)(2,1)S(1)} %reshape.101), channel_id=1, replica_groups=mesh['ep'=32,'dp'=4] {'ep'}, dimensions={0} | all-to-all | bytes 3932160 | tf_op jit(solution)/shard_map/all_to_all | solution.py:78
  172.3 3.7 %stack.3 = bf16[4,640,1536]{2,1,0:T(8,128)(2,1)} broadcast(bf16[640,1536]{1,0:T(8,128)(2,1)S(1)} %copy-done.4), dimensions={1,2} | broadcast | bytes 9830400 | tf_op jit(solution)/shard_map/stack | solution.py:84
  176.0 5.7 %all-to-all-start.4 = ((bf16[4,640,1536]{2,1,0:T(8,128)(2,1)}), bf16[4,640,1536]{2,1,0:T(8,128)(2,1)}, u32[]{:S(2)}, u32[]{:S(2)}) async-start(bf16[4,640,1536]{2,1,0:T(8,128)(2,1)} %stack.3), calls=%async_computation.4 | async-start | bytes 15728640 | tf_op jit(solution)/shard_map/all_to_all | solution.py:84
  184.3 85.7 %all-to-all-done.4 = bf16[4,640,1536]{2,1,0:T(8,128)(2,1)} async-done(((bf16[4,640,1536]{2,1,0:T(8,128)(2,1)}), bf16[4,640,1536]{2,1,0:T(8,128)(2,1)}, u32[]{:S(2)}, u32[]{:S(2)}) %all-to-all-start.4) | async-done | bytes 7864352 | tf_op jit(solution)/shard_map/all_to_all | solution.py:84
  269.9 9.7 %fusion.28 = f32[2560,384]{1,0:T(8,128)} fusion(bf16[2560,1536]{1,0:T(8,128)(2,1)} %bitcast.8, bf16[1,1536,1536]{2,1,0:T(8,128)(2,1)} %param.17, s32[]{:T(128)S(6)} %select_n.2), kind=kOutput, calls=%fused_computation.44 | convolution fusion | flops 3019898880 | bytes 12976132 | tf_op jit(solution)/shard_map/dot_general | solution.py:10
  279.6 7.7 %convolution_add_fusion = f32[2560,384]{1,0:T(8,128)S(1)} fusion(bf16[2560,1536]{1,0:T(8,128)(2,1)} %all-gather.2.cloned.1.call-done, bf16[1,1536,1536]{2,1,0:T(8,128)(2,1)} %param.16, s32[]{:T(128)S(6)} %select_n.2), kind=kOutput, calls=%fused_computation.10 | convolution fusion | flops 3020881920 | bytes 12976132 | tf_op jit(solution)/shard_map/dot_general | solution.py:10
  287.3 5.6 %fusion.25 = f32[2560,384]{1,0:T(8,128)S(1)} fusion(bf16[2560,1536]{1,0:T(8,128)(2,1)S(1)} %copy-done.7, bf16[1,1536,1536]{2,1,0:T(8,128)(2,1)} %param.15, s32[]{:T(128)S(6)} %select_n.2), kind=kOutput, calls=%fused_computation.41 | convolution fusion | flops 3019898880 | bytes 12976132 | tf_op jit(solution)/shard_map/dot_general | solution.py:10
  292.9 7.9 %fusion.16 = bf16[1,384,1536]{2,1,0:T(8,128)(2,1)} fusion(bf16[2560,1536]{1,0:T(8,128)(2,1)} %bitcast.8, f32[2560,384]{1,0:T(8,128)S(1)} %convolution_add_fusion, f32[2560,384]{1,0:T(8,128)S(1)} %fusion.25), kind=kOutput, calls=%fused_computation.29 | convolution fusion | flops 3027369984 | bytes 16908288 | tf_op jit(solution)/shard_map/dot_general | solution.py:16
  300.8 4.5 %fusion.14 = bf16[1,384,1536]{2,1,0:T(8,128)(2,1)} fusion(bf16[2560,1536]{1,0:T(8,128)(2,1)S(1)} %copy-done.7, f32[2560,384]{1,0:T(8,128)S(1)} %copy-done.8, f32[2560,384]{1,0:T(8,128)S(1)} %convolution_add_fusion, f32[2560,384]{1,0:T(8,128)S(1)} %fusion.25), kind=kOutput, calls=%fused_computation.27 | convolution fusion | flops 3031302144 | bytes 20840448 | tf_op jit(solution)/shard_map/dot_general | solution.py:16
  305.4 4.4 %fusion.15 = bf16[1,384,1536]{2,1,0:T(8,128)(2,1)} fusion(bf16[2560,1536]{1,0:T(8,128)(2,1)S(1)} %copy-done.7, f32[2560,384]{1,0:T(8,128)S(1)} %copy-done.8, f32[2560,384]{1,0:T(8,128)S(1)} %fusion.25), kind=kOutput, calls=%fused_computation.28 | convolution fusion | flops 3027369984 | bytes 16908288 | tf_op jit(solution)/shard_map/dot_general | solution.py:16
  (55 shorter events, 14.6 us)
Async XLA Ops:
  7.2 6.4 %copy-start = (bf16[128,1536]{1,0:T(8,128)(2,1)S(1)}, bf16[128,1536]{1,0:T(8,128)(2,1)}, u32[]{:S(2)}) copy-start(bf16[128,1536]{1,0:T(8,128)(2,1)} %param.10) | copy-start | bytes 1179652
  16.3 40.9 %all-to-all-start.1 = ((bf16[32,20,1536]{2,1,0:T(8,128)(2,1)}), bf16[32,20,1536]{2,1,0:T(8,128)(2,1)S(1)}, u32[]{:S(2)}, u32[]{:S(2)}) async-start(bf16[32,20,1536]{2,1,0:T(8,128)(2,1)} %reshape.99), calls=%async_computation.1 | async-start | bytes 4718592 | tf_op jit(solution)/shard_map/all_to_all | solution.py:78
  57.3 37.6 %all-to-all-start = ((bf16[32,20,1536]{2,1,0:T(8,128)(2,1)}), bf16[32,20,1536]{2,1,0:T(8,128)(2,1)}, u32[]{:S(2)}, u32[]{:S(2)}) async-start(bf16[32,20,1536]{2,1,0:T(8,128)(2,1)} %reshape.97), calls=%async_computation | async-start | bytes 4718592 | tf_op jit(solution)/shard_map/all_to_all | solution.py:78
  63.6 216.0 %all-gather.2.cloned.1.call-start = ((), (), s32[]{:S(2)}) async-start(), calls=%async_computation.5 | async-start | bytes 9830400 | tf_op jit(solution)/shard_map/all_gather | solution.py:81
  65.6 8.3 %slice-start = ((s8[4718592]{0:T(1024)(128)(4,1)}), s8[524288]{0:T(1024)(128)(4,1)S(1)}, s32[]{:S(2)}) async-start(s8[4718592]{0:T(1024)(128)(4,1)} %bitcast.62), calls=%async_computation.6 | async-start | bytes 1048576
  65.6 8.3 %copy-start.5 = (bf16[640,1536]{1,0:T(8,128)(2,1)S(1)}, bf16[640,1536]{1,0:T(8,128)(2,1)}, u32[]{:S(2)}) copy-start(bf16[640,1536]{1,0:T(8,128)(2,1)} %reshape.100) | copy-start | bytes 5898244
  65.6 8.3 %slice-start.1 = ((s8[4718592]{0:T(1024)(128)(4,1)}), s8[4194304]{0:T(1024)(128)(4,1)S(1)}, s32[]{:S(2)}) async-start(s8[4718592]{0:T(1024)(128)(4,1)} %bitcast.62), calls=%async_computation.7 | async-start | bytes 8388608
  97.4 10.9 %copy-start.3 = (bf16[640,1536]{1,0:T(8,128)(2,1)}, bf16[640,1536]{1,0:T(8,128)(2,1)S(1)}, u32[]{:S(2)}) copy-start(bf16[640,1536]{1,0:T(8,128)(2,1)S(1)} %reshape.98) | copy-start | bytes 5898244
  109.0 24.3 %all-to-all-start.3 = ((bf16[32,1,20]{2,1,0:T(2,128)(2,1)}), bf16[32,1,20]{2,1,0:T(2,128)(2,1)S(1)}, u32[]{:S(2)}, u32[]{:S(2)}) async-start(bf16[32,1,20]{2,1,0:T(2,128)(2,1)} %convert_element_type.97), calls=%async_computation.3 | async-start | bytes 32768 | tf_op jit(solution)/shard_map/all_to_all | solution.py:78
  114.7 9.1 %copy-start.9 = (f32[640,1536]{1,0:T(8,128)S(1)}, f32[640,1536]{1,0:T(8,128)}, u32[]{:S(2)}) copy-start(f32[640,1536]{1,0:T(8,128)} %fusion.2) | copy-start | bytes 11796484
  114.7 9.1 %copy-start.10 = (f32[640,1536]{1,0:T(8,128)S(1)}, f32[640,1536]{1,0:T(8,128)}, u32[]{:S(2)}) copy-start(f32[640,1536]{1,0:T(8,128)} %get-tuple-element.12) | copy-start | bytes 11796484
  133.4 38.9 %copy-start.4 = (bf16[640,1536]{1,0:T(8,128)(2,1)S(1)}, bf16[640,1536]{1,0:T(8,128)(2,1)}, u32[]{:S(2)}) copy-start(bf16[640,1536]{1,0:T(8,128)(2,1)} %copy-done.3) | copy-start | bytes 5898244
  176.0 6.1 %copy-start.6 = (f32[128,4]{0,1:T(4,128)S(1)}, f32[128,4]{0,1:T(4,128)}, u32[]{:S(2)}) copy-start(f32[128,4]{0,1:T(4,128)} %param.11) | copy-start | bytes 6148
  176.0 6.7 %copy-start.2 = (bf16[32,20,1536]{2,1,0:T(8,128)(2,1)S(1)}, bf16[32,20,1536]{2,1,0:T(8,128)(2,1)}, u32[]{:S(2)}) copy-start(bf16[32,20,1536]{2,1,0:T(8,128)(2,1)} %all_to_all.29) | copy-start | bytes 5898244
  176.0 93.9 %all-to-all-start.4 = ((bf16[4,640,1536]{2,1,0:T(8,128)(2,1)}), bf16[4,640,1536]{2,1,0:T(8,128)(2,1)}, u32[]{:S(2)}, u32[]{:S(2)}) async-start(bf16[4,640,1536]{2,1,0:T(8,128)(2,1)} %stack.3), calls=%async_computation.4 | async-start | bytes 15728640 | tf_op jit(solution)/shard_map/all_to_all | solution.py:84
  279.6 7.7 %copy-start.7 = (bf16[2560,1536]{1,0:T(8,128)(2,1)S(1)}, bf16[2560,1536]{1,0:T(8,128)(2,1)}, u32[]{:S(2)}) copy-start(bf16[2560,1536]{1,0:T(8,128)(2,1)} %all-gather.2.cloned.1.call-done) | copy-start | bytes 23592964
  292.9 7.9 %copy-start.8 = (f32[2560,384]{1,0:T(8,128)S(1)}, f32[2560,384]{1,0:T(8,128)}, u32[]{:S(2)}) copy-start(f32[2560,384]{1,0:T(8,128)} %fusion.28) | copy-start | bytes 11796484
  305.4 4.4 %copy-start.1 = (bf16[128,1536]{1,0:T(8,128)(2,1)S(1)}, bf16[128,1536]{1,0:T(8,128)(2,1)}, u32[]{:S(2)}) copy-start(bf16[128,1536]{1,0:T(8,128)(2,1)} %param.10) | copy-start | bytes 1179652
Sparse Core Ops, SparseCore 0:
  66.0 79.8 all-gather.1
